TPU v7x, 512 devices: a whole 4x8x8 slice. The times are simulated.
512 devices in a mesh: tm: 8 (over y_hi, x), height: 64 (over y_lo, z, core).
Axes of the slice: x: 4, y: 8 (y_hi: 2, y_lo: 4; y = y_hi * 4 + y_lo), z: 8, core: 2. Of those that a mesh axis runs over, the one named last changes fastest.
Arguments:
- pixels: bfloat16 [16, 3, 512, 1024], P('tm', None, 'height'), may hold values from -6 to 6
- conv_weight: bfloat16 [3, 3, 3, 48, 128], replicated, may hold values from -0.15625 to 0.15625
- conv_bias: float32 [128], replicated, may hold values from -3 to 3
- down_weight: bfloat16 [2, 2, 128, 256], replicated, may hold values from -0.25 to 0.25
- down_bias: float32 [256], replicated, may hold values from -3 to 3
- cotangent: bfloat16 [16, 64, 128, 256], P('tm', 'height'), may hold values from -6 to 6
Outputs:
- features: bfloat16 [16, 64, 128, 256], P('tm', 'height')
- grad_conv: float32 [3, 3, 3, 48, 128], replicated
- grad_conv_bias: float32 [128], replicated
- grad_down: float32 [2, 2, 128, 256], replicated
- grad_down_bias: float32 [256], replicated
- grad_pixels: float32 [16, 3, 512, 1024], P('tm', None, 'height')
All inputs are finite; a program needn't handle non-finite values.
Results may differ from a plain program's by a relative error of at most 0.012.
Values may be sent and summed in bfloat16 or wider, within the bound.
A program may use at most 64 MiB of HBM per device.

v0:
```python
import math

import jax
import jax.numpy as jnp
import numpy as np
from jax import lax
from jax.sharding import PartitionSpec as P

haar_matrix = (
    np.kron(np.array([[1.0, 1.0], [1.0, -1.0]]), np.array([[1.0, 1.0], [1.0, -1.0]])) * 0.5
)


def extended_2(shard, sides, width):
    for axis, dim in sides:
        size, length = (lax.axis_size(axis), shard.shape[dim])
        up = [(i, (i + 1) % size) for i in range(size - 1)]
        down = [(j, i) for i, j in up]
        last = lax.slice_in_dim(shard, length - width, length, axis=dim)
        first = lax.slice_in_dim(shard, 0, width, axis=dim)
        before = lax.ppermute(last, axis, up)
        after = lax.ppermute(first, axis, down)
        shard = jnp.concatenate([before, shard, after], axis=dim)
    return shard


def passed_along(value, axis, steps):
    count = lax.axis_size(axis)
    first, last = (max(0, -steps), min(count, count - steps))
    return lax.ppermute(value, axis, [(source, source + steps) for source in range(first, last)])


def analyse(pixels):
    frame_count, colors, height_px, width_px = pixels.shape
    table = jnp.asarray(haar_matrix, jnp.float32)
    blocks = pixels.astype(jnp.float32).reshape(
        frame_count, colors, height_px // 4, 4, width_px // 4, 4
    )
    result = jnp.einsum("fkrucv,iu,jv->fkijrc", blocks, table, table)
    return result.reshape(frame_count, colors * 16, height_px // 4, width_px // 4)


def synthesise(dcoeffs):
    frame_count, channels, height_cells, width_cells = dcoeffs.shape
    table = jnp.asarray(haar_matrix, jnp.float32)
    parts = dcoeffs.reshape(frame_count, channels // 16, 4, 4, height_cells, width_cells)
    result = jnp.einsum("fkijrc,iu,jv->fkrucv", parts, table, table)
    return result.reshape(frame_count, channels // 16, height_cells * 4, width_cells * 4)


def all_taps():
    return [
        (tap_time, tap_row, tap_col)
        for tap_time in range(3)
        for tap_row in range(3)
        for tap_col in range(3)
    ]


def local(pixels, conv_weight, conv_bias, down_weight, down_bias, cotangent):
    frame_count = pixels.shape[0]
    height_cells = pixels.shape[2] // 4
    width_cells = pixels.shape[3] // 4
    channels = conv_weight.shape[3]
    outer = conv_weight.shape[4]
    coeffs = analyse(pixels).astype(jnp.bfloat16)
    tall = extended_2(coeffs, (("height", 2),), 1)
    earlier = passed_along(tall, "tm", 1)
    extended = jnp.pad(jnp.concatenate([earlier, tall], axis=0), ((0, 0), (0, 0), (0, 0), (1, 1)))
    pre = jnp.zeros((frame_count, height_cells, width_cells, outer), jnp.float32) + conv_bias
    for tap_time, tap_row, tap_col in all_taps():
        window = extended[
            tap_time : tap_time + frame_count,
            :,
            tap_row : tap_row + height_cells,
            tap_col : tap_col + width_cells,
        ]
        pre = pre + jnp.einsum(
            "fkrc,ko->frco",
            window,
            conv_weight[tap_time, tap_row, tap_col],
            preferred_element_type=jnp.float32,
        )
    act = jax.nn.silu(pre).astype(jnp.bfloat16)
    grouped = act.reshape(frame_count, height_cells // 2, 2, width_cells // 2, 2, outer)
    features = (
        jnp.einsum("fqupvk,uvko->fqpo", grouped, down_weight, preferred_element_type=jnp.float32)
        + down_bias
    ).astype(jnp.bfloat16)
    dact = jnp.einsum(
        "fqpo,uvko->fqupvk", cotangent, down_weight, preferred_element_type=jnp.float32
    )
    dact = dact.reshape(frame_count, height_cells, width_cells, outer)
    sig = jax.nn.sigmoid(pre)
    slope = (dact * sig * (1.0 + pre * (1.0 - sig))).astype(jnp.bfloat16)
    local_down = jnp.einsum(
        "fqupvk,fqpo->uvko", grouped, cotangent, preferred_element_type=jnp.float32
    )
    local_down_bias = jnp.sum(cotangent.astype(jnp.float32), axis=(0, 1, 2))
    pieces = []
    for tap_time, tap_row, tap_col in all_taps():
        window = extended[
            tap_time : tap_time + frame_count,
            :,
            tap_row : tap_row + height_cells,
            tap_col : tap_col + width_cells,
        ]
        pieces.append(
            jnp.einsum("fkrc,frco->ko", window, slope, preferred_element_type=jnp.float32)
        )
    local_conv = jnp.stack(pieces).reshape(3, 3, 3, channels, outer)
    local_conv_bias = jnp.sum(slope.astype(jnp.float32), axis=(0, 1, 2))
    summed = lax.psum((local_conv, local_conv_bias, local_down, local_down_bias), ("tm", "height"))
    count = frame_count * lax.axis_size("tm") * height_cells * lax.axis_size("height") * width_cells
    scale = 1.0 / math.sqrt(count)
    grad_conv = scale * summed[0]
    grad_conv_bias = scale * summed[1]
    grad_down = scale * summed[2]
    grad_down_bias = scale * summed[3]
    slope_tall = extended_2(slope, (("height", 1),), 1)
    following = passed_along(slope_tall, "tm", -1)
    later = jnp.pad(
        jnp.concatenate([slope_tall, following], axis=0), ((0, 0), (0, 0), (1, 1), (0, 0))
    )
    dcoeffs = jnp.zeros((frame_count, channels, height_cells, width_cells), jnp.float32)
    for tap_time, tap_row, tap_col in all_taps():
        window = later[
            2 - tap_time : 2 - tap_time + frame_count,
            2 - tap_row : 2 - tap_row + height_cells,
            2 - tap_col : 2 - tap_col + width_cells,
        ]
        dcoeffs = dcoeffs + jnp.einsum(
            "frco,ko->fkrc",
            window,
            conv_weight[tap_time, tap_row, tap_col],
            preferred_element_type=jnp.float32,
        )
    grad_pixels = synthesise(dcoeffs)
    return (features, grad_conv, grad_conv_bias, grad_down, grad_down_bias, grad_pixels)


def solution(mesh):
    return jax.shard_map(
        local,
        mesh=mesh,
        in_specs=(P("tm", None, "height", None), P(), P(), P(), P(), P("tm", "height", None, None)),
        out_specs=(
            P("tm", "height", None, None),
            P(),
            P(),
            P(),
            P(),
            P("tm", None, "height", None),
        ),
        check_vma=False,
    )
```

profile of v0, /device:TPU:1, one launch (start us, length us, event | category | flops | bytes accessed | tf_op | source)
XLA Modules:
  0.0 377.7 jit_solution(16497143423366269262)
XLA Ops:
  7.2 8.5 %reshape.49 = bf16[2,3,2,4,256,4]{5,4,3,2,1,0:T(8,128)(2,1)} reshape(bf16[2,3,8,1024]{3,2,1,0:T(8,128)(2,1)} %param.8) | data formatting | bytes 196608 | tf_op jit(solution)/shard_map/reshape | solution.py:36
  15.7 3.3 copy.34
  19.7 5.4 %collective-permute-start = (bf16[2,48,1,256]{3,1,2,0:T(8,128)(2,1)S(1)}, bf16[2,48,1,256]{3,1,2,0:T(8,128)(2,1)S(1)}, u32[]{:S(2)}, u32[]{:S(2)}) collective-permute-start(bf16[2,48,1,256]{3,1,2,0:T(8,128)(2,1)S(1)} %copy.115), channel_id=1, source_target_pairs={{0,1},{1,2},{2,3},{3,4},{4,5},{5,6},{6,7},{7,8},{8,9},{9,10},{10,1... | collective-permute-start | bytes 147464 | tf_op jit(solution)/shard_map/ppermute | solution.py:21
  25.1 4.7 %collective-permute-start.1 = (bf16[2,48,1,256]{3,1,2,0:T(8,128)(2,1)S(1)}, bf16[2,48,1,256]{3,1,2,0:T(8,128)(2,1)S(1)}, u32[]{:S(2)}, u32[]{:S(2)}) collective-permute-start(bf16[2,48,1,256]{3,1,2,0:T(8,128)(2,1)S(1)} %copy.116), channel_id=1, source_target_pairs={{1,0},{2,1},{3,2},{4,3},{5,4},{6,5},{7,6},{8,7},{9,8},{10,9},{11,1... | collective-permute-start | bytes 147464 | tf_op jit(solution)/shard_map/ppermute | solution.py:22
  29.8 0.8 collective-permute-done.1
  30.6 3.0 collective-permute-start.2
  33.9 0.4 copy.27
  34.4 2.8 collective-permute-done.2
  44.9 0.3 convolution_add_fusion.9
  45.3 0.3 convolution_add_fusion.8
  45.7 0.5 convert_reduce_fusion
  46.6 2.4 collective-permute-start.3
  49.0 2.0 collective-permute-start.4
  56.5 1.1 convolution_bitcast_fusion
  57.6 115.5 %all-reduce.2 = (f32[128]{0:T(128)S(1)}, f32[256]{0:T(256)S(1)}) all-reduce(f32[128]{0:T(128)S(1)} %get-tuple-element.22, f32[256]{0:T(256)S(1)} %convert_reduce_fusion.1), channel_id=1, replica_groups=mesh['tm'=8,'height'=64] {'tm','height'}, use_global_device_ids=true, to_apply=%region_2.3 | all-reduce | flops 384 | bytes 3072 | tf_op jit(solution)/shard_map/psum | solution.py:113
  173.1 0.6 broadcast_multiply_fusion.2
  173.7 0.5 broadcast_multiply_fusion.3
  174.3 1.5 collective-permute-start.5
  175.8 0.9 fusion.36
  176.7 172.8 %all-reduce.6.cloned.1.call-done = (f32[3,3,3,48,128]{4,3,2,1,0:T(8,128)}, f32[2,2,128,256]{3,2,1,0:T(8,128)}) async-done(((f32[3,3,3,48,128]{4,3,2,1,0:T(8,128)}, f32[2,2,128,256]{3,2,1,0:T(8,128)}), (f32[3,3,3,48,128]{4,3,2,1,0:T(8,128)}, f32[2,2,128,256]{3,2,1,0:T(8,128)})) %all-reduce.6.cloned.1.call-update) | async-done | bytes 1187856 | tf_op jit(solution)/shard_map/psum | solution.py:113
  349.5 1.9 broadcast_multiply_fusion.1
  351.3 2.0 broadcast_multiply_fusion
  359.6 4.0 %copy.31 = f32[2,3,2,4,256,4]{5,4,3,2,1,0:T(8,128)} copy(f32[2,3,2,4,256,4]{4,5,2,1,0,3:T(4,128)S(1)} %convolution_bitcast_fusion.5) | data formatting | bytes 393216 | tf_op jit(solution)/shard_map/fkijrc,iu,jv->fkrucv/transpose | solution.py:47
  363.6 7.3 %reshape.55 = f32[2,3,8,1024]{3,2,1,0:T(8,128)} reshape(f32[2,3,2,4,256,4]{5,4,3,2,1,0:T(8,128)} %copy.31) | data formatting | bytes 393216 | tf_op jit(solution)/shard_map/reshape | solution.py:48
  (116 shorter events, 20.5 us)
Async XLA Ops:
  7.2 26.5 %copy-start = (bf16[2,2,128,256]{3,2,1,0:T(8,128)(2,1)S(1)}, bf16[2,2,128,256]{3,2,1,0:T(8,128)(2,1)}, u32[]{:S(2)}) copy-start(bf16[2,2,128,256]{3,2,1,0:T(8,128)(2,1)} %param.11) | copy-start | bytes 786436
  7.2 342.3 %all-reduce.6.cloned.1.call-start = ((), (), s32[]{:S(2)}) async-start(), calls=%async_computation | async-start | bytes 2375680 | tf_op jit(solution)/shard_map/psum | solution.py:113
  15.7 3.3 copy-start.4
  15.7 17.9 %copy-start.1 = (bf16[2,1,128,256]{3,2,1,0:T(8,128)(2,1)S(1)}, bf16[2,1,128,256]{3,2,1,0:T(8,128)(2,1)}, u32[]{:S(2)}) copy-start(bf16[2,1,128,256]{3,2,1,0:T(8,128)(2,1)} %param.13) | copy-start | bytes 393220
  19.5 17.7 %copy-start.2 = (bf16[3,3,3,48,128]{4,3,2,1,0:T(8,128)(2,1)S(1)}, bf16[3,3,3,48,128]{4,3,2,1,0:T(8,128)(2,1)}, u32[]{:S(2)}) copy-start(bf16[3,3,3,48,128]{4,3,2,1,0:T(8,128)(2,1)} %param.9) | copy-start | bytes 995332
  19.7 10.1 %collective-permute-start = (bf16[2,48,1,256]{3,1,2,0:T(8,128)(2,1)S(1)}, bf16[2,48,1,256]{3,1,2,0:T(8,128)(2,1)S(1)}, u32[]{:S(2)}, u32[]{:S(2)}) collective-permute-start(bf16[2,48,1,256]{3,1,2,0:T(8,128)(2,1)S(1)} %copy.115), channel_id=1, source_target_pairs={{0,1},{1,2},{2,3},{3,4},{4,5},{5,6},{6,7},{7,8},{8,9},{9,10},{10,1... | collective-permute-start | bytes 147464 | tf_op jit(solution)/shard_map/ppermute | solution.py:21
  25.1 5.5 %collective-permute-start.1 = (bf16[2,48,1,256]{3,1,2,0:T(8,128)(2,1)S(1)}, bf16[2,48,1,256]{3,1,2,0:T(8,128)(2,1)S(1)}, u32[]{:S(2)}, u32[]{:S(2)}) collective-permute-start(bf16[2,48,1,256]{3,1,2,0:T(8,128)(2,1)S(1)} %copy.116), channel_id=1, source_target_pairs={{1,0},{2,1},{3,2},{4,3},{5,4},{6,5},{7,6},{8,7},{9,8},{10,9},{11,1... | collective-permute-start | bytes 147464 | tf_op jit(solution)/shard_map/ppermute | solution.py:22
  30.6 6.5 %collective-permute-start.2 = (bf16[2,48,4,256]{3,1,2,0:T(8,128)(2,1)S(1)}, bf16[2,48,4,256]{3,1,2,0:T(8,128)(2,1)S(1)}, u32[]{:S(2)}, u32[]{:S(2)}) collective-permute-start(bf16[2,48,4,256]{3,1,2,0:T(8,128)(2,1)S(1)} %get-tuple-element.33), channel_id=1, source_target_pairs={{0,64},{64,128},{128,192},{192,256},{256,320},{320,384},{384,448},... | collective-permute-start | bytes 589832 | tf_op jit(solution)/shard_map/ppermute | solution.py:30
  40.7 1.8 copy-start.5
  46.6 127.6 %collective-permute-start.3 = (bf16[2,1,256,128]{3,2,1,0:T(8,128)(2,1)S(1)}, bf16[2,1,256,128]{3,2,1,0:T(8,128)(2,1)S(1)}, u32[]{:S(2)}, u32[]{:S(2)}) collective-permute-start(bf16[2,1,256,128]{3,2,1,0:T(8,128)(2,1)S(1)} %get-tuple-element.25), channel_id=1, source_target_pairs={{0,1},{1,2},{2,3},{3,4},{4,5},{5,6},{6,7},{7,8},{8,9},{9,10},{10,1... | collective-permute-start | bytes 393224 | tf_op jit(solution)/shard_map/ppermute | solution.py:21
  49.0 125.2 %collective-permute-start.4 = (bf16[2,1,256,128]{3,2,1,0:T(8,128)(2,1)S(1)}, bf16[2,1,256,128]{3,2,1,0:T(8,128)(2,1)S(1)}, u32[]{:S(2)}, u32[]{:S(2)}) collective-permute-start(bf16[2,1,256,128]{3,2,1,0:T(8,128)(2,1)S(1)} %get-tuple-element.26), channel_id=1, source_target_pairs={{1,0},{2,1},{3,2},{4,3},{5,4},{6,5},{7,6},{8,7},{9,8},{10,9},{11,1... | collective-permute-start | bytes 393224 | tf_op jit(solution)/shard_map/ppermute | solution.py:22
  56.1 119.7 %copy-start.6 = (f32[256]{0:T(256)S(1)}, f32[256]{0:T(256)}, u32[]{:S(2)}) copy-start(f32[256]{0:T(256)} %param.12) | copy-start | bytes 3076
  56.5 1.1 copy-start.3
  174.3 179.1 %collective-permute-start.5 = (bf16[2,4,256,128]{3,2,1,0:T(8,128)(2,1)S(1)}, bf16[2,4,256,128]{3,2,1,0:T(8,128)(2,1)S(1)}, u32[]{:S(2)}, u32[]{:S(2)}) collective-permute-start(bf16[2,4,256,128]{3,2,1,0:T(8,128)(2,1)S(1)} %pad_maximum_fusion.1), channel_id=1, source_target_pairs={{64,0},{128,64},{192,128},{256,192},{320,256},{384,320},{448,384},... | collective-permute-start | bytes 1572872 | tf_op jit(solution)/shard_map/ppermute | solution.py:30
Sparse Core Ops, SparseCore 0:
  57.8 291.6 all-reduce.5
where the time goes:
time: 378 us
  waiting for transfers between devices  176 us (47%)
  blocking collectives  115 us (30%)
  local copies, waits for them, and re-layouts  23.8 us (6%)
  matrix products  23 us (6%)
  starting transfers between devices  18.9 us (5%)
  between operations  14.9 us (4%)
  other arithmetic  5.21 us (1%)
    psum x1, waiting for transfers between devices, local(): lax.psum((local_conv, local_conv_bias, local_down, local_down_bias), ('tm...  173 us
    psum x1, blocking collectives, local(): lax.psum((local_conv, local_conv_bias, local_down, local_down_bias), ('tm...  115 us
    reshape x2, local copies, waits for them, and re-layouts, analyse(): pixels.astype(jnp.float32)  11.8 us
    dot_general x27, matrix products, local(): jnp.einsum('fkrc,ko->frco', window, conv_weight[tap_time, tap_row, tap_co...  8.72 us
    ppermute x2, starting transfers between devices, extended_2(): before = lax.ppermute(last, axis, up)  7.74 us
  transfers between devices with their start and end apart: 7, of which 3 were waited for; matrix products, arithmetic and copies ran while one was open for 3% of the time, Pallas kernels for 0%

commit v1 on v0

v1 whole, which is shorter than its diff:
```python
import functools
import math

import jax
import jax.numpy as jnp
from jax import lax
from jax.experimental import pallas as pl
from jax.experimental.pallas import tpu as pltpu
from jax.sharding import PartitionSpec as P

MESH = pl.DeviceIdType.MESH
F32 = jnp.float32
BF16 = jnp.bfloat16

FACTORS = {"y_hi": 2, "x": 4, "y_lo": 4, "z": 8}

TAPS = 27 * 48
BAND = 9 * 48
CELL = 3 * 48
GRAD_ROWS = TAPS + 1024 + 24


def dot(a, b, contract):
    return lax.dot_general(a, b, (contract, ((), ())), preferred_element_type=F32)


NN = ((1,), (0,))
NT = ((1,), (1,))
TN = ((0,), (0,))


def to_right(value):
    even, odd = value[:, :128], value[:, 128:]
    lane = lax.broadcasted_iota(jnp.int32, even.shape, 1)
    moved = jnp.where(lane == 127, 0.0, pltpu.roll(even, 127, axis=1))
    return odd, moved


def to_left(value):
    even, odd = value[:, :128], value[:, 128:]
    lane = lax.broadcasted_iota(jnp.int32, even.shape, 1)
    moved = jnp.where(lane == 0, 0.0, pltpu.roll(odd, 1, axis=1))
    return moved, even


def butterfly(parts):
    p0, p1, p2, p3 = parts
    a, b, c, d = p0 + p1, p0 - p1, p2 + p3, p2 - p3
    return a + c, b + d, a - c, b - d


def main_kernel(
    fac, m,
    px, w, cb_ref, dw, db_ref, cot,
    feat, gp, gath,
    wt, haar, y32, c32, cext, shifted, acc, dact, act, slope,
    grads, csend, crecv, p1, xsend, xrecv, p2, ysend, yrecv, zbuf,
    esend, erecv, e32, tsend, trecv, ef,
    hs_sem, hr_sem, es_sem, er_sem,
    cs_sem, cr_sem, xs_sem, xr_sem, ys_sem, yr_sem, zs_sem, zr_sem,
    ay_s, ay_r, ax_s, ax_r, ac_s, ac_r,
):
    X, Y0, Z = fac["x"], fac["y_lo"], fac["z"]
    NY = fac["y_hi"] * Y0
    T, H = fac["y_hi"] * X, Y0 * Z * 2
    tm, h = lax.axis_index("tm"), lax.axis_index("height")
    core = lax.rem(h, 2)
    z = lax.rem(lax.div(h, 2), Z)
    y_lo = lax.div(h, 2 * Z)
    x = lax.rem(tm, X)
    y = lax.div(tm, X) * Y0 + y_lo
    other = 1 - core

    def dev(x_, y_, z_, c_):
        return (lax.div(y_, Y0) * X + x_, lax.rem(y_, Y0) * (2 * Z) + z_ * 2 + c_)

    partner = dev(x, y, z, other)
    xs = [lax.rem(x + d, X) for d in range(1, X)]
    ys = [lax.rem(y + d, NY) for d in range(1, NY)]
    zs = [lax.rem(z + d, Z) for d in range(1, Z)]
    xdev = [dev(v, y, z, core) for v in xs]
    ydev = [dev(x, v, z, core) for v in ys]
    zdev = [dev(x, y, v, core) for v in zs]
    up, down = (tm, lax.rem(h + H - 1, H)), (tm, lax.rem(h + 1, H))
    prev, nxt = (lax.rem(tm + T - 1, T), h), (lax.rem(tm + 1, T), h)
    has_up, has_down, has_prev, has_next = h > 0, h < H - 1, tm > 0, tm < T - 1

    barrier = pltpu.get_barrier_semaphore()
    for peer in [partner] + xdev + ydev + zdev:
        pl.semaphore_signal(barrier, inc=1, device_id=peer, device_id_type=MESH)
    for there, peer in ((has_up, up), (has_down, down), (has_prev, prev), (has_next, nxt)):

        @pl.when(there)
        def _(peer=peer):
            pl.semaphore_signal(barrier, inc=1, device_id=peer, device_id_type=MESH)

    def remote(src, dst, send, recv, peer):
        return pltpu.make_async_remote_copy(
            src_ref=src, dst_ref=dst, send_sem=send, recv_sem=recv,
            device_id=peer, device_id_type=MESH,
        )

    for block in range(4):
        row = lax.broadcasted_iota(jnp.int32, (256, 256), 0) + 256 * block
        col = lax.broadcasted_iota(jnp.int32, (256, 256), 1)
        hit = (row >> 3 == (col & 127)) & (((row >> 2) & 1) == (col >> 7))
        base = jnp.where(hit, 0.25, 0.0)
        low = (1 - 2 * (row & 1)).astype(F32)
        high = (1 - (row & 2)).astype(F32)
        for j, value in enumerate((base, base * low, base * high, base * low * high)):
            haar[256 * block : 256 * (block + 1), 256 * j : 256 * (j + 1)] = value.astype(BF16)

    stacked = jnp.concatenate(
        [px[f, k].astype(F32) for k in range(3) for f in range(2)], axis=0
    ).astype(BF16)
    value = dot(stacked, haar[...], NN)
    for n in range(8):
        y32[n] = value[:, 128 * n : 128 * (n + 1)]
    for k in range(3):
        for n in range(8):
            rows = butterfly([y32[n, pl.ds(16 * k + u, 4, stride=4), :] for u in range(4)])
            for i in range(4):
                at = 16 * k + 4 * i + n // 2
                c32[n % 2, pl.ds(at, 4, stride=48), :] = rows[i]
    for f in range(2):
        for r in range(2):
            at = (2 * f + r) * 48
            for e in range(2):
                cext[2 + f, 1 + r, :, 128 * e : 128 * (e + 1)] = c32[e, at : at + 48, :].astype(BF16)

    expected = (
        1 + (X - 1) + (NY - 1) + (Z - 1)
        + has_up.astype(jnp.int32) + has_down.astype(jnp.int32)
        + has_prev.astype(jnp.int32) + has_next.astype(jnp.int32)
    )
    pl.semaphore_wait(barrier, expected)

    to_next = remote(cext.at[2:4, 1:3], cext.at[0:2, 1:3], hs_sem.at[0], hr_sem.at[0], nxt)
    own_down = remote(cext.at[2:4, 2], cext.at[2:4, 0], hs_sem.at[1], hr_sem.at[1], down)
    own_up = remote(cext.at[2:4, 1], cext.at[2:4, 3], hs_sem.at[2], hr_sem.at[2], up)
    far_down = remote(cext.at[0:2, 2], cext.at[0:2, 0], hs_sem.at[3], hr_sem.at[3], down)
    far_up = remote(cext.at[0:2, 1], cext.at[0:2, 3], hs_sem.at[4], hr_sem.at[4], up)

    @pl.when(has_next)
    def _():
        to_next.start()

    @pl.when(has_down)
    def _():
        own_down.start()

    @pl.when(has_up)
    def _():
        own_up.start()

    @pl.when(h == 0)
    def _():
        for f in range(4):
            cext[f, 0] = jnp.zeros((48, 256), BF16)

    @pl.when(h == H - 1)
    def _():
        for f in range(4):
            cext[f, 3] = jnp.zeros((48, 256), BF16)

    @pl.when(tm == 0)
    def _():
        for f in range(2):
            for r in range(4):
                cext[f, r] = jnp.zeros((48, 256), BF16)

    def shift(f, r):
        block = cext[f, r]
        wide = block.astype(F32)
        left, right = to_left(wide), to_right(wide)
        shifted[f, r, 0:48, 0:128] = left[0].astype(BF16)
        shifted[f, r, 0:48, 128:256] = left[1].astype(BF16)
        shifted[f, r, 48:96, :] = block
        shifted[f, r, 96:144, 0:128] = right[0].astype(BF16)
        shifted[f, r, 96:144, 128:256] = right[1].astype(BF16)

    for a in range(3):
        wt[a] = w[BAND * a : BAND * (a + 1), :].astype(F32).T.astype(BF16)
    for f in range(2):
        for r in range(2):
            for e in range(2):
                at = 128 * (2 * r + e)
                dact[f, r, :, 128 * e : 128 * (e + 1)] = dot(dw[at : at + 128, :], cot[f], NT)
    for f in range(2):
        for r in range(2):
            shift(2 + f, 1 + r)

    def taps(f, r):
        return shifted[f, r : r + 3].reshape(BAND, 256)

    @pl.when(has_up)
    def _():
        own_down.wait_recv()

    @pl.when(has_down)
    def _():
        own_up.wait_recv()

    for f in range(2):
        shift(2 + f, 0)
        shift(2 + f, 3)
    for r in range(2):
        acc[0, r] = dot(wt[2], taps(2, r), NN)
        acc[1, r] = dot(wt[1], taps(2, r), NN) + dot(wt[2], taps(3, r), NN)

    @pl.when(has_prev)
    def _():
        to_next.wait_recv()

        @pl.when(has_down)
        def _():
            far_down.start()

        @pl.when(has_up)
        def _():
            far_up.start()

    for f in range(2):
        for r in range(2):
            shift(f, 1 + r)

    @pl.when(has_prev & has_up)
    def _():
        far_down.wait_recv()

    @pl.when(has_prev & has_down)
    def _():
        far_up.wait_recv()

    for f in range(2):
        shift(f, 0)
        shift(f, 3)

    bias = cb_ref[...]
    for f in range(2):
        for r in range(2):
            pre = acc[f, r] + bias
            if f == 0:
                pre = pre + (dot(wt[0], taps(0, r), NN) + dot(wt[1], taps(1, r), NN))
            else:
                pre = pre + dot(wt[0], taps(1, r), NN)
            sig = jax.nn.sigmoid(pre)
            act[f, r] = (pre * sig).astype(BF16)
            slope[f, r] = (dact[f, r] * sig * (1.0 + pre * (1.0 - sig))).astype(BF16)

    half = X * NY * m

    def put(at, value):
        count = value.shape[0]
        first = max(0, min(count, half - at))
        if first:
            grads[0, at : at + first, :] = value[:first]
        if first < count:
            start = at + first - half
            grads[1, start : start + count - first, :] = value[first:]

    for a in range(3):
        total = None
        for f in range(2):
            for r in range(2):
                part = dot(taps(f + a, r), slope[f, r], NT)
                total = part if total is None else total + part
        put(BAND * a, total)
    for u in range(2):
        for v in range(2):
            total = dot(act[0, u, :, 128 * v : 128 * (v + 1)], cot[0], NN) + dot(
                act[1, u, :, 128 * v : 128 * (v + 1)], cot[1], NN
            )
            at = TAPS + 128 * (2 * u + v)
            put(at, total[:, :128])
            put(at + 512, total[:, 128:])
    ones = jnp.ones((8, 256), BF16)
    total = None
    for f in range(2):
        for r in range(2):
            part = dot(ones, slope[f, r], NT)
            total = part if total is None else total + part
    put(TAPS + 1024, total)
    total = dot(ones[:, :128], cot[0], NN) + dot(ones[:, :128], cot[1], NN)
    put(TAPS + 1032, total[:, :128])
    put(TAPS + 1040, total[:, 128:])
    if GRAD_ROWS < 2 * half:
        put(GRAD_ROWS, jnp.zeros((2 * half - GRAD_ROWS, 128), F32))

    csend[...] = grads[other].reshape(X, NY, m, 128).astype(BF16)
    to_partner = remote(csend, crecv, cs_sem.at[0], cr_sem.at[0], partner)
    to_partner.start()

    for f in range(2):
        total = None
        for u in range(2):
            for v in range(2):
                at = 128 * (2 * u + v)
                part = dot(act[f, u, :, 128 * v : 128 * (v + 1)], dw[at : at + 128, :], TN)
                total = part if total is None else total + part
        feat[f] = (total + db_ref[...]).astype(BF16)

    to_partner.wait_recv()
    total = grads[core].reshape(X, NY, m, 128) + crecv[...].astype(F32)
    p1[...] = total
    xsend[...] = total.astype(BF16)
    to_x = [
        remote(xsend.at[v], xrecv.at[i], xs_sem.at[i], xr_sem.at[i], xdev[i])
        for i, v in enumerate(xs)
    ]
    for c in to_x:
        c.start()

    def dcoeffs(fe, re):
        total = None
        for f in range(2):
            for r in range(2):
                a, b = fe - f, re - r
                if 0 <= a < 3 and 0 <= b < 3:
                    at = CELL * (3 * a + b)
                    part = dot(w[at : at + CELL, :], slope[f, r], NN)
                    total = part if total is None else total + part
        right = to_right(total[0:48])
        left = to_left(total[96:144])
        mid = total[48:96]
        return mid[:, :128] + right[0] + left[0], mid[:, 128:] + right[1] + left[1]

    for fe in range(4):
        for i, re in enumerate((0, 3)):
            even, odd = dcoeffs(fe, re)
            esend[i, fe, :, 0:128] = even.astype(BF16)
            esend[i, fe, :, 128:256] = odd.astype(BF16)
    e_up = remote(esend.at[0], erecv.at[0], es_sem.at[0], er_sem.at[0], up)
    e_down = remote(esend.at[1], erecv.at[1], es_sem.at[1], er_sem.at[1], down)

    @pl.when(has_up)
    def _():
        e_up.start()

    @pl.when(has_down)
    def _():
        e_down.start()

    for fe in range(4):
        for re in range(2):
            even, odd = dcoeffs(fe, re + 1)
            e32[fe, re, :, 0:128] = even
            e32[fe, re, :, 128:256] = odd

    for c in to_x:
        c.wait_recv()
    total = p1[x]
    for i in range(X - 1):
        total = total + xrecv[i].astype(F32)
    p2[...] = total
    ysend[...] = total.astype(BF16)
    to_y = [
        remote(ysend.at[v], yrecv.at[i], ys_sem.at[i], yr_sem.at[i], ydev[i])
        for i, v in enumerate(ys)
    ]
    for c in to_y:
        c.start()

    @pl.when(has_down)
    def _():
        e_up.wait_recv()
        for fe in range(4):
            e32[fe, 1] = e32[fe, 1] + erecv[0, fe].astype(F32)

    @pl.when(has_up)
    def _():
        e_down.wait_recv()
        for fe in range(4):
            e32[fe, 0] = e32[fe, 0] + erecv[1, fe].astype(F32)

    for fe in range(2):
        for re in range(2):
            tsend[fe, re] = e32[fe, re].astype(BF16)

    for c in to_y:
        c.wait_recv()
    total = p2[y]
    for i in range(NY - 1):
        total = total + yrecv[i].astype(F32)
    zbuf[z] = total.astype(BF16)
    to_z = [
        remote(zbuf.at[z], zbuf.at[z], zs_sem.at[i], zr_sem.at[i], zdev[i]) for i in range(Z - 1)
    ]
    for c in to_z:
        c.start()

    to_prev = remote(tsend, trecv, es_sem.at[2], er_sem.at[2], prev)

    @pl.when(has_prev)
    def _():
        to_prev.start()

    for c in to_z:
        c.wait_recv()
    total = zbuf[0].astype(F32)
    for i in range(1, Z):
        total = total + zbuf[i].astype(F32)
    gath[core, x, y] = total.astype(BF16)

    all_y = [
        remote(gath.at[core, x, y], gath.at[core, x, y], ay_s.at[i], ay_r.at[i], ydev[i])
        for i in range(NY - 1)
    ]
    for c in all_y:
        c.start()

    def synthesis():
        for f in range(2):
            for r in range(2):
                at = (2 * f + r) * 48
                for e in range(2):
                    ef[e, at : at + 48, :] = e32[2 + f, r, :, 128 * e : 128 * (e + 1)]

        @pl.when(has_next)
        def _():
            to_prev.wait_recv()
            for f in range(2):
                for r in range(2):
                    at = (2 * f + r) * 48
                    for e in range(2):
                        more = trecv[f, r, :, 128 * e : 128 * (e + 1)].astype(F32)
                        ef[e, at : at + 48, :] = ef[e, at : at + 48, :] + more

        for k in range(3):
            for n in range(8):
                rows = butterfly(
                    [ef[n % 2, pl.ds(16 * k + 4 * i + n // 2, 4, stride=48), :] for i in range(4)]
                )
                for u in range(4):
                    y32[n, pl.ds(16 * k + u, 4, stride=4), :] = rows[u]
        value = jnp.concatenate([y32[n] for n in range(8)], axis=1)
        high = value.astype(BF16)
        low = (value - high.astype(F32)).astype(BF16)
        both = dot(jnp.concatenate([high, low], axis=0), haar[...], NT)
        result = both[:48] + both[48:]
        for k in range(3):
            for f in range(2):
                at = 16 * k + 8 * f
                gp[f, k] = result[at : at + 8]

    for c in all_y:
        c.wait_recv()
    all_x = [
        remote(gath.at[core, x], gath.at[core, x], ax_s.at[i], ax_r.at[i], xdev[i])
        for i in range(X - 1)
    ]
    for c in all_x:
        c.start()
    back = [x] + [lax.rem(x + X - d, X) for d in range(1, X)]
    all_c = [
        remote(gath.at[core, v], gath.at[core, v], ac_s.at[i], ac_r.at[i], partner)
        for i, v in enumerate(back)
    ]
    all_c[0].start()
    synthesis()
    for i in range(1, X):
        all_x[i - 1].wait_recv()
        all_c[i].start()
    for i in range(X):
        all_c[i].wait_recv()

    @pl.when(has_next)
    def _():
        to_next.wait_send()

    @pl.when(has_down)
    def _():
        own_down.wait_send()
        e_down.wait_send()

    @pl.when(has_up)
    def _():
        own_up.wait_send()
        e_up.wait_send()

    @pl.when(has_prev & has_down)
    def _():
        far_down.wait_send()

    @pl.when(has_prev & has_up)
    def _():
        far_up.wait_send()

    @pl.when(has_prev)
    def _():
        to_prev.wait_send()

    to_partner.wait_send()
    for c in to_x + to_y + to_z + all_y + all_x + all_c:
        c.wait_send()


def finish_kernel(scale, g_ref, gc_ref, gcb_ref, gd_ref, gdb_ref):
    value = g_ref[...].astype(F32)
    value = value.reshape(-1, 128) * scale
    gc_ref[...] = value[:TAPS]
    gd_ref[:, 0:128] = value[TAPS : TAPS + 512]
    gd_ref[:, 128:256] = value[TAPS + 512 : TAPS + 1024]
    gcb_ref[...] = value[TAPS + 1024 : TAPS + 1025]
    gdb_ref[:, 0:128] = value[TAPS + 1032 : TAPS + 1033]
    gdb_ref[:, 128:256] = value[TAPS + 1040 : TAPS + 1041]


def local(pixels, conv_weight, conv_bias, down_weight, down_bias, cotangent):
    fac = FACTORS
    X, Z = fac["x"], fac["z"]
    NY = fac["y_hi"] * fac["y_lo"]
    pieces = 2 * X * NY
    m = -(-GRAD_ROWS // (8 * pieces)) * 8
    vmem = pltpu.VMEM
    dma = pltpu.SemaphoreType.DMA
    inside = pl.BlockSpec(memory_space=vmem)
    scratch = [
        vmem((3, 128, BAND), BF16),
        vmem((1024, 1024), BF16),
        vmem((8, 48, 128), F32),
        vmem((2, 192, 128), F32),
        vmem((4, 4, 48, 256), BF16),
        vmem((4, 4, CELL, 256), BF16),
        vmem((2, 2, 128, 256), F32),
        vmem((2, 2, 128, 256), F32),
        vmem((2, 2, 128, 256), BF16),
        vmem((2, 2, 128, 256), BF16),
        vmem((2, X * NY * m, 128), F32),
        vmem((X, NY, m, 128), BF16),
        vmem((X, NY, m, 128), BF16),
        vmem((X, NY, m, 128), F32),
        vmem((X, NY, m, 128), BF16),
        vmem((X - 1, NY, m, 128), BF16),
        vmem((NY, m, 128), F32),
        vmem((NY, m, 128), BF16),
        vmem((NY - 1, m, 128), BF16),
        vmem((Z, m, 128), BF16),
        vmem((2, 4, 48, 256), BF16),
        vmem((2, 4, 48, 256), BF16),
        vmem((4, 2, 48, 256), F32),
        vmem((2, 2, 48, 256), BF16),
        vmem((2, 2, 48, 256), BF16),
        vmem((2, 192, 128), F32),
        dma((5,)), dma((5,)), dma((3,)), dma((3,)),
        dma((1,)), dma((1,)), dma((X - 1,)), dma((X - 1,)),
        dma((NY - 1,)), dma((NY - 1,)), dma((Z - 1,)), dma((Z - 1,)),
        dma((NY - 1,)), dma((NY - 1,)), dma((X - 1,)), dma((X - 1,)),
        dma((X,)), dma((X,)),
    ]
    features, grad_pixels, gathered = pl.pallas_call(
        functools.partial(main_kernel, fac, m),
        out_shape=(
            jax.ShapeDtypeStruct((2, 128, 256), BF16),
            jax.ShapeDtypeStruct((2, 3, 8, 1024), F32),
            jax.ShapeDtypeStruct((2, X, NY, m, 128), BF16),
        ),
        in_specs=[inside] * 6,
        out_specs=(inside,) * 3,
        scratch_shapes=scratch,
        compiler_params=pltpu.CompilerParams(
            collective_id=0, has_side_effects=True, vmem_limit_bytes=48 * 1024 * 1024
        ),
        name="front",
    )(
        pixels,
        conv_weight.reshape(TAPS, 128),
        conv_bias.reshape(128, 1),
        down_weight.reshape(512, 256),
        down_bias.reshape(1, 256),
        cotangent.reshape(2, 128, 256),
    )
    count = 2 * lax.axis_size("tm") * 2 * lax.axis_size("height") * 256
    grad_conv, grad_conv_bias, grad_down, grad_down_bias = pl.pallas_call(
        functools.partial(finish_kernel, 1.0 / math.sqrt(count)),
        out_shape=(
            jax.ShapeDtypeStruct((TAPS, 128), F32),
            jax.ShapeDtypeStruct((1, 128), F32),
            jax.ShapeDtypeStruct((512, 256), F32),
            jax.ShapeDtypeStruct((1, 256), F32),
        ),
        in_specs=[inside],
        out_specs=(inside,) * 4,
        compiler_params=pltpu.CompilerParams(vmem_limit_bytes=16 * 1024 * 1024),
        name="finish",
    )(gathered)
    return (
        features.reshape(2, 1, 128, 256),
        grad_conv.reshape(3, 3, 3, 48, 128),
        grad_conv_bias.reshape(128),
        grad_down.reshape(2, 2, 128, 256),
        grad_down_bias.reshape(256),
        grad_pixels,
    )


def solution(mesh):
    return jax.shard_map(
        local,
        mesh=mesh,
        in_specs=(P("tm", None, "height", None), P(), P(), P(), P(), P("tm", "height", None, None)),
        out_specs=(
            P("tm", "height", None, None),
            P(),
            P(),
            P(),
            P(),
            P("tm", None, "height", None),
        ),
        check_vma=False,
    )
```

time: 378 us -> 65 us (0.17)
  waiting for transfers between devices: 176 us -> 0 us
  blocking collectives: 115 us -> 0 us
  Pallas kernels: 0 us -> 57.7 us
  matrix products: 23 us -> 0 us
  starting transfers between devices: 18.9 us -> 0 us
  local copies, waits for them, and re-layouts: 23.8 us -> 6.38 us
  between operations: 14.9 us -> 0.66 us
  other arithmetic: 5.21 us -> 0 us
    psum x1 -> x0, waiting for transfers between devices: 173 us -> none  [local(): lax.psum((local_conv, local_conv_bias, local_down, local_down_bias), ('tm...]
    psum x1 -> x0, blocking collectives: 115 us -> none  [local(): lax.psum((local_conv, local_conv_bias, local_down, local_down_bias), ('tm...]
    pallas_call x0 -> x2, Pallas kernels: none -> 57.7 us  [the longest x1 56.6 us: local(): pl.pallas_call(functools.partial(main_kernel, fac, m), out_shape=(jax.Sha...]
    dot_general x88 -> x0, matrix products: 23 us -> none  [the longest x27 8.72 us: local(): jnp.einsum('fkrc,ko->frco', window, conv_weight[tap_time, tap_row, tap_co...]
    reshape x4 -> x1, local copies, waits for them, and re-layouts: 19.1 us -> 0.11 us  [local(): conv_bias.reshape(128, 1)]
    ppermute x6 -> x0, starting transfers between devices: 18.9 us -> none  [the longest x2 7.74 us: extended_2(): before = lax.ppermute(last, axis, up)]
    unnamed x18 -> x14, local copies, waits for them, and re-layouts: 0.1 us -> 6.26 us
    mul x4 -> x0, other arithmetic: 4.95 us -> none  [the longest x1 1.99 us: local(): grad_conv = scale * summed[0]]
  transfers between devices with their start and end apart: 7 -> 0, of which waited for: 3 -> 0; matrix products, arithmetic and copies ran while one was open for 3% -> 0% of each run, Pallas kernels for 0% -> 0%
where the time goes in v1:
time: 65 us; the launch traced here: 64.7 us
  Pallas kernels  57.7 us (89%)
  local copies, waits for them, and re-layouts  6.38 us (10%)
  between operations  0.66 us (1%)
    pallas_call x1, Pallas kernels, local(): pl.pallas_call(functools.partial(main_kernel, fac, m), out_shape=(jax.Sha...  56.6 us
    unnamed x14, local copies, waits for them, and re-layouts  6.26 us

profile of v1, /device:TPU:1, one launch (start us, length us, event | category | flops | bytes accessed | tf_op | source)
XLA Modules:
  0.0 64.7 jit_solution(9763495340646674280)
XLA Ops:
  0.6 0.0 copy-start.5
  0.6 0.6 copy-done.5
  1.3 0.0 copy-start.4
  1.3 0.1 copy.12.cb_ref
  1.4 0.6 copy-done.4
  2.0 0.0 copy-start
  2.0 1.0 %copy-done = bf16[3,3,3,48,128]{4,3,2,1,0:T(8,128)(2,1)S(1)} copy-done((bf16[3,3,3,48,128]{4,3,2,1,0:T(8,128)(2,1)S(1)}, bf16[3,3,3,48,128]{4,3,2,1,0:T(8,128)(2,1)}, u32[]{:S(2)}) %copy-start) | copy-done | bytes 331800
  2.9 0.0 copy-start.1
  2.9 0.9 %copy-done.1 = bf16[2,2,128,256]{3,2,1,0:T(8,128)(2,1)S(1)} copy-done((bf16[2,2,128,256]{3,2,1,0:T(8,128)(2,1)S(1)}, bf16[2,2,128,256]{3,2,1,0:T(8,128)(2,1)}, u32[]{:S(2)}) %copy-start.1) | copy-done | bytes 262168
  3.9 0.0 copy-start.2
  3.9 0.9 %copy-done.2 = bf16[2,1,128,256]{3,2,1,0:T(8,128)(2,1)S(1)} copy-done((bf16[2,1,128,256]{3,2,1,0:T(8,128)(2,1)S(1)}, bf16[2,1,128,256]{3,2,1,0:T(8,128)(2,1)}, u32[]{:S(2)}) %copy-start.2) | copy-done | bytes 131096
  4.8 0.0 copy-start.3
  4.8 0.9 %copy-done.3 = bf16[2,3,8,1024]{3,2,1,0:T(8,128)(2,1)S(1)} copy-done((bf16[2,3,8,1024]{3,2,1,0:T(8,128)(2,1)S(1)}, bf16[2,3,8,1024]{3,2,1,0:T(8,128)(2,1)}, u32[]{:S(2)}) %copy-start.3) | copy-done | bytes 98328
  5.7 56.6 %front.1 = (bf16[2,128,256]{2,1,0:T(8,128)(2,1)S(1)}, f32[2,3,8,1024]{3,2,1,0:T(8,128)S(1)}, bf16[2,4,8,40,128]{4,3,2,1,0:T(8,128)(2,1)S(1)}) custom-call(bf16[2,3,8,1024]{3,2,1,0:T(8,128)(2,1)S(1)} %copy-done.3, bf16[1296,128]{1,0:T(8,128)(2,1)S(1)} %bitcast.12, f32[128,1]{1,0:T(8,128)S(1)} %copy.12.cb_ref, bf16[512,256]{1,0:T(8,128)(2,1)S(1)} %bitcast.13, ...), custom_call_target="tpu_custom_call" | custom-call | tf_op jit(solution)/shard_map/front/pallas_call | solution.py:551
  62.3 1.1 %finish.1 = (f32[1296,128]{1,0:T(8,128)}, f32[1,128]{1,0:T(1,128)}, f32[512,256]{1,0:T(8,128)}, f32[1,256]{1,0:T(1,128)}) custom-call(bf16[2,4,8,40,128]{4,3,2,1,0:T(8,128)(2,1)S(1)} %get-tuple-element.14.g_ref), custom_call_target="tpu_custom_call" | custom-call | tf_op jit(solution)/shard_map/finish/pallas_call | solution.py:574
  63.4 0.7 %copy.16 = bf16[2,1,128,256]{3,2,1,0:T(8,128)(2,1)} copy(bf16[2,1,128,256]{3,2,1,0:T(8,128)(2,1)S(1)} %bitcast.14) | data formatting | bytes 262144
  64.0 0.7 %copy.17 = f32[2,3,8,1024]{3,2,1,0:T(8,128)} copy(f32[2,3,8,1024]{3,2,1,0:T(8,128)S(1)} %get-tuple-element.37) | data formatting | bytes 393216
Async XLA Ops:
  0.6 0.7 %copy-start.5 = (f32[128]{0:T(128)S(1)}, f32[128]{0:T(128)}, u32[]{:S(2)}) copy-start(f32[128]{0:T(128)} %param.8) | copy-start | bytes 1540
  1.3 0.7 %copy-start.4 = (f32[256]{0:T(256)S(1)}, f32[256]{0:T(256)}, u32[]{:S(2)}) copy-start(f32[256]{0:T(256)} %param.10) | copy-start | bytes 3076
  2.0 1.0 %copy-start = (bf16[3,3,3,48,128]{4,3,2,1,0:T(8,128)(2,1)S(1)}, bf16[3,3,3,48,128]{4,3,2,1,0:T(8,128)(2,1)}, u32[]{:S(2)}) copy-start(bf16[3,3,3,48,128]{4,3,2,1,0:T(8,128)(2,1)} %param.7) | copy-start | bytes 995332
  2.9 0.9 %copy-start.1 = (bf16[2,2,128,256]{3,2,1,0:T(8,128)(2,1)S(1)}, bf16[2,2,128,256]{3,2,1,0:T(8,128)(2,1)}, u32[]{:S(2)}) copy-start(bf16[2,2,128,256]{3,2,1,0:T(8,128)(2,1)} %param.9) | copy-start | bytes 786436
  3.9 0.9 %copy-start.2 = (bf16[2,1,128,256]{3,2,1,0:T(8,128)(2,1)S(1)}, bf16[2,1,128,256]{3,2,1,0:T(8,128)(2,1)}, u32[]{:S(2)}) copy-start(bf16[2,1,128,256]{3,2,1,0:T(8,128)(2,1)} %param.11) | copy-start | bytes 393220
  4.8 0.9 %copy-start.3 = (bf16[2,3,8,1024]{3,2,1,0:T(8,128)(2,1)S(1)}, bf16[2,3,8,1024]{3,2,1,0:T(8,128)(2,1)}, u32[]{:S(2)}) copy-start(bf16[2,3,8,1024]{3,2,1,0:T(8,128)(2,1)} %px.1) | copy-start | bytes 294916
